TPU v7x, 32 devices: a whole 2x2x4 slice. The times are simulated.
32 devices in a mesh: groups: 2 (over y), gx: 4 (over z), gy: 4 (over x, core).
Axes of the slice: x: 2, y: 2, z: 4, core: 2. Of those that a mesh axis runs over, the one named last changes fastest.
Arguments:
- thermal_deviation: float32 [32, 256, 512], P('groups', 'gy', 'gx'), parts along dimension 0, may hold values from -6 to 6
- brine_content: float32 [32, 256, 512], P('groups', 'gy', 'gx'), parts along dimension 0, may hold values from 0.2 to 2.4
- current_components: float32 [4, 16, 256, 512], P('groups', None, 'gy', 'gx'), parts along dimension 0, may hold values from -4 to 4
- sea_indicator: int32 [256, 512], P('gy', 'gx'), may hold values from 0 to 1, as said below
- flooded_layer_number: int32 [256, 512], P('gy', 'gx'), may hold values from 1 to 16
- footprint_square_metres: float32 [256, 512], P('gy', 'gx'), may hold values from 0.5 to 5
- rainfall_input: float32 [256, 512], P('gy', 'gx'), may hold values from -2 to 3.5
- seam_partner_index: int32 [512], P('gx'), may hold values from 0 to 511, as said below
Outputs:
- temperature_next: float32 [32, 256, 512], P('groups', 'gy', 'gx'), parts along dimension 0
- salinity_next: float32 [32, 256, 512], P('groups', 'gy', 'gx'), parts along dimension 0
There are 2 independent parts, one for each index of `groups`. A program takes and returns all parts, laid end to end along the dimension named above; an argument that names none is the same for every part. Nothing has to cross between parts.
Inputs may be any that keep to these rules, and one draw needn't show every extreme that they name: `sea_indicator`: at least one column is ocean. seam_partner_index[x] = (s - x) mod 512 for one s of each draw with s mod 128 = 127; the map is its own inverse and has no fixed point.
All inputs are finite; a program needn't handle non-finite values.
Results may differ from a plain program's by a relative error of at most 0.00002.
Values sent between devices are 32-bit elements; how exact they have to be, the bound alone decides.
A program may use at most 64 MiB of HBM per device.

v0:
```python
import jax
import jax.numpy as jnp
from jax import lax
from jax.sharding import PartitionSpec as P

time_step = 0.25
diffusivity = 0.5
vertical_mixing = 0.3
top_thickness = 0.5


def with_halo(cells, sides, width, closed):
    for axis, dim in sides:
        count = lax.axis_size(axis)
        ends = count if closed else count - 1
        head = lax.slice_in_dim(cells, 0, width, axis=dim)
        tail = lax.slice_in_dim(cells, cells.shape[dim] - width, cells.shape[dim], axis=dim)
        cells = jnp.concatenate(
            [
                lax.ppermute(tail, axis, [(i, (i + 1) % count) for i in range(ends)]),
                cells,
                lax.ppermute(head, axis, [((i + 1) % count, i) for i in range(ends)]),
            ],
            axis=dim,
        )
    return cells


def face_flux(near_cells, far_cells, face_speed, near_wet, far_wet):
    upwind = jnp.maximum(face_speed, 0.0) * near_cells + jnp.minimum(face_speed, 0.0) * far_cells
    return near_wet * far_wet * (upwind - diffusivity * (far_cells - near_cells))


def wet_from(depth_plane, layer_stack_number):
    level_index = jnp.arange(layer_stack_number, dtype=jnp.float32)
    return (level_index[:, None, None] < depth_plane[None]).astype(jnp.float32)


def split_tracer(block_planes, layer_stack_number):
    return block_planes[: 2 * layer_stack_number].reshape(
        (2, layer_stack_number) + block_planes.shape[1:]
    )


def shards(
    thermal_deviation,
    brine_content,
    current_components,
    sea_indicator,
    flooded_layer_number,
    footprint_square_metres,
    rainfall_input,
    seam_partner_index,
):
    layer_stack_number, parallel_total_number, meridian_total_number = thermal_deviation.shape
    stacked_layer_number = (sea_indicator * flooded_layer_number).astype(jnp.float32)
    wet_area = footprint_square_metres * sea_indicator.astype(jnp.float32)
    surface = brine_content[0]
    total_area, total_fresh, salt_fresh, salt_only = lax.psum(
        (
            jnp.sum(wet_area),
            jnp.sum(wet_area * rainfall_input),
            jnp.sum(wet_area * surface * rainfall_input),
            jnp.sum(wet_area * surface),
        ),
        ("gx", "gy"),
    )
    mean_fresh = total_fresh / total_area
    balanced = rainfall_input - mean_fresh
    total_salt = salt_fresh - mean_fresh * salt_only
    virtual = -surface * balanced + total_salt / total_area
    top_row = jnp.concatenate(
        [
            thermal_deviation[:, -1, :],
            brine_content[:, -1, :],
            current_components[1][:, -1, :],
            stacked_layer_number[-1:, :],
        ],
        axis=0,
    )
    gathered = lax.all_gather(top_row, "gx", axis=1, tiled=True)
    partner_row = jnp.take(gathered, seam_partner_index, axis=1)
    partner_fields = jnp.concatenate(
        [partner_row[: 2 * layer_stack_number], partner_row[3 * layer_stack_number :]], axis=0
    )
    partner_speed = partner_row[2 * layer_stack_number : 3 * layer_stack_number]
    is_top = lax.axis_index("gy") == lax.axis_size("gy") - 1
    planes = jnp.concatenate(
        [
            thermal_deviation,
            brine_content,
            current_components[0],
            current_components[1],
            stacked_layer_number[None],
        ],
        axis=0,
    )
    zonal_padded = with_halo(planes, (("gx", 2),), 1, True)
    meridional_padded = with_halo(planes, (("gy", 1),), 1, False)
    zonal_tracer = split_tracer(zonal_padded, layer_stack_number)
    zonal_wet = wet_from(zonal_padded[4 * layer_stack_number], layer_stack_number)
    zonal_near_speed = zonal_padded[2 * layer_stack_number : 3 * layer_stack_number][..., :-1]
    halo_top = jnp.concatenate(
        [
            meridional_padded[: 2 * layer_stack_number, -1, :],
            meridional_padded[4 * layer_stack_number :, -1, :],
        ],
        axis=0,
    )
    above_fields = jnp.where(is_top, partner_fields, halo_top)
    upper_tracer_cells = jnp.concatenate(
        [
            meridional_padded[: 2 * layer_stack_number, 1:-1, :],
            above_fields[: 2 * layer_stack_number, None, :],
        ],
        axis=1,
    )
    upper_depth = jnp.concatenate(
        [
            meridional_padded[4 * layer_stack_number, 1:-1, :],
            above_fields[2 * layer_stack_number][None, :],
        ],
        axis=0,
    )
    lower_cells = meridional_padded[:, :-1, :]
    lower_tracer = split_tracer(lower_cells, layer_stack_number)
    lower_wet = wet_from(lower_cells[4 * layer_stack_number], layer_stack_number)
    upper_tracer = split_tracer(upper_tracer_cells, layer_stack_number)
    upper_wet = wet_from(upper_depth, layer_stack_number)
    north_speed = lower_cells[3 * layer_stack_number : 4 * layer_stack_number]
    carried_quantity = jnp.stack([thermal_deviation, brine_content])
    wet_cells = wet_from(stacked_layer_number, layer_stack_number)
    zonal_flux = face_flux(
        zonal_tracer[..., :-1],
        zonal_tracer[..., 1:],
        zonal_near_speed,
        zonal_wet[..., :-1],
        zonal_wet[..., 1:],
    )
    fold_speed = 0.5 * (north_speed[:, -1, :] - partner_speed)
    last_speed = jnp.where(is_top, fold_speed, north_speed[:, -1, :])
    north_speed = jnp.concatenate([north_speed[:, :-1, :], last_speed[:, None, :]], axis=1)
    meridional_flux = face_flux(lower_tracer, upper_tracer, north_speed, lower_wet, upper_wet)
    vertical = (
        wet_cells[:-1]
        * wet_cells[1:]
        * vertical_mixing
        * (carried_quantity[:, :-1] - carried_quantity[:, 1:])
    )
    zero_layer = jnp.zeros_like(vertical[:, :1])
    from_above = jnp.concatenate([zero_layer, vertical], axis=1)
    to_below = jnp.concatenate([vertical, zero_layer], axis=1)
    tendency = time_step / footprint_square_metres * (
        zonal_flux[..., :-1]
        - zonal_flux[..., 1:]
        + meridional_flux[:, :, :-1]
        - meridional_flux[:, :, 1:]
    ) + time_step * (from_above - to_below)
    updated = carried_quantity + wet_cells * tendency
    surface_next = updated[1, 0] + time_step / top_thickness * virtual * wet_cells[0]
    salinity_next = jnp.concatenate([surface_next[None], updated[1, 1:]], axis=0)
    return (updated[0], salinity_next)


def solution(mesh):
    in_specs = (
        P("groups", "gy", "gx"),
        P("groups", "gy", "gx"),
        P("groups", None, "gy", "gx"),
        P("gy", "gx"),
        P("gy", "gx"),
        P("gy", "gx"),
        P("gy", "gx"),
        P("gx"),
    )
    out_specs = (P("groups", "gy", "gx"), P("groups", "gy", "gx"))
    return jax.shard_map(shards, mesh=mesh, in_specs=in_specs, out_specs=out_specs, check_vma=False)
```

profile of v0, /device:TPU:0, one launch (start us, length us, event | category | flops | bytes accessed | tf_op | source)
XLA Modules:
  0.0 111.4 jit_solution(16813490816440808588)
XLA Ops:
  0.6 2.3 %constant_dynamic-update-slice_fusion.2 = (f32[65,64,128]{2,0,1:T(8,128)S(1)}, f32[16,64,128]{2,0,1:T(8,128)}) fusion(f32[16,64,128]{2,1,0:T(8,128)} %param.8), kind=kLoop, calls=%fused_computation.82 | loop fusion | bytes 1572864
  3.1 1.1 %constant_dynamic-update-slice_fusion.1 = (f32[65,64,128]{2,0,1:T(8,128)S(1)}, f32[16,64,128]{2,0,1:T(8,128)}) fusion(f32[65,64,128]{2,0,1:T(8,128)S(1)} %get-tuple-element.22, f32[16,64,128]{2,1,0:T(8,128)S(1)} %copy-done.2), kind=kLoop, calls=%fused_computation.81 | loop fusion | bytes 1572864
  5.0 2.9 %fusion.24 = (f32[65,64,1]{2,0,1:T(8,128)}, f32[65,64,1]{2,0,1:T(8,128)}) fusion(f32[65,64,128]{2,0,1:T(8,128)S(1)} %dynamic-update-slice.4), kind=kLoop, calls=%fused_computation.87 | loop fusion | bytes 66560 | tf_op jit(solution)/shard_map/slice | solution.py:17
  7.9 3.1 %copy.160 = f32[65,64,1]{0,1,2:T(8,128)} copy(f32[65,64,1]{2,0,1:T(8,128)} %get-tuple-element.14) | data formatting | bytes 33280 | tf_op jit(solution)/shard_map/slice | solution.py:17
  11.0 3.1 %collective-permute-start = (f32[65,64,1]{0,1,2:T(8,128)}, f32[65,64,1]{0,1,2:T(8,128)}, u32[]{:S(2)}, u32[]{:S(2)}) collective-permute-start(f32[65,64,1]{0,1,2:T(8,128)} %copy.160), channel_id=1, source_target_pairs={{0,4},{4,8},{8,12},{12,0},{1,5},{5,9},{9,13},{13,1},{2,6},{6,10},{... | collective-permute-start | bytes 49928 | tf_op jit(solution)/shard_map/ppermute | solution.py:20
  14.0 3.1 %copy.161 = f32[65,64,1]{0,1,2:T(8,128)} copy(f32[65,64,1]{2,0,1:T(8,128)} %get-tuple-element.15) | data formatting | bytes 33280 | tf_op jit(solution)/shard_map/slice | solution.py:16
  17.1 2.1 %collective-permute-start.1 = (f32[65,64,1]{0,1,2:T(8,128)}, f32[65,64,1]{0,1,2:T(8,128)}, u32[]{:S(2)}, u32[]{:S(2)}) collective-permute-start(f32[65,64,1]{0,1,2:T(8,128)} %copy.161), channel_id=1, source_target_pairs={{4,0},{8,4},{12,8},{0,12},{5,1},{9,5},{13,9},{1,13},{6,2},{10,6},{... | collective-permute-start | bytes 49928 | tf_op jit(solution)/shard_map/ppermute | solution.py:22
  19.2 0.6 fusion.25
  19.8 1.3 %collective-permute-start.2 = (f32[65,1,128]{2,0,1:T(8,128)}, f32[65,1,128]{2,0,1:T(8,128)}, u32[]{:S(2)}, u32[]{:S(2)}) collective-permute-start(f32[65,1,128]{2,0,1:T(8,128)} %get-tuple-element.17), channel_id=1, source_target_pairs={{1,0},{2,1},{3,2},{5,4},{6,5},{7,6},{9,8},{10,9},{11,10},{13,12},{... | collective-permute-start | bytes 99848 | tf_op jit(solution)/shard_map/ppermute | solution.py:22
  21.1 3.6 %collective-permute-start.3 = (f32[65,1,128]{2,0,1:T(8,128)}, f32[65,1,128]{2,0,1:T(8,128)}, u32[]{:S(2)}, u32[]{:S(2)}) collective-permute-start(f32[65,1,128]{2,0,1:T(8,128)} %get-tuple-element.16), channel_id=1, source_target_pairs={{0,1},{1,2},{2,3},{4,5},{5,6},{6,7},{8,9},{9,10},{10,11},{12,13},{... | collective-permute-start | bytes 99848 | tf_op jit(solution)/shard_map/ppermute | solution.py:20
  24.7 1.3 %copy.203 = f32[1,16,64,128]{3,1,2,0:T(8,128)S(1)} copy(f32[1,16,64,128]{3,2,1,0:T(8,128)} %copy-done.5) | data formatting | bytes 1048576
  26.1 0.7 compare_select_fusion
  26.8 0.5 compare_and_fusion
  27.3 1.1 pad_maximum_fusion.6
  28.4 0.8 fusion.11
  29.2 0.7 slice_bitcast_fusion.7
  29.9 0.7 slice_bitcast_fusion.5
  30.6 13.3 %all_gather.3 = f32[49,512]{1,0:T(8,128)S(1)} all-gather(f32[49,128]{1,0:T(8,128)S(1)} %pad_maximum_fusion.11), channel_id=1, replica_groups=mesh['groups'=2,'gx'=4,'gy'=4] {'gx'}, dimensions={1}, use_global_device_ids=true | all-gather | bytes 125440 | tf_op jit(solution)/shard_map/all_gather | solution.py:81
  43.9 0.8 copy.172
  44.8 0.7 pad_clamp_fusion
  45.4 1.6 %gather_fusion = f32[128,49]{1,0:T(8,128)S(1)} fusion(f32[49,512]{0,1:T(8,128)} %copy.172, s32[1024]{0:T(1024)S(1)} %pad_clamp_fusion), kind=kCustom, calls=%fused_computation | custom fusion | bytes 50688 | tf_op jit(solution)/shard_map/jit(_take)/gather | solution.py:82
  47.0 0.7 copy.173
  47.7 2.0 %fusion.12 = f32[15,64,128]{2,1,0:T(8,128)} fusion(f32[16,64,128]{2,1,0:T(8,128)} %fusion.11), kind=kLoop, calls=%fused_computation.45 | loop fusion | flops 245760 | bytes 1474560 | tf_op jit(solution)/shard_map/mul | solution.py:145
  49.8 0.8 convert_multiply_fusion
  50.6 1.4 %select_bitcast_fusion = f32[49,128]{1,0:T(8,128)} fusion(f32[128,49]{0,1:T(8,128)} %copy.173, pred[128]{0:T(512)(128)(4,1)} %compare_and_fusion), kind=kLoop, calls=%fused_computation.68 | loop fusion | flops 6272 | bytes 50304 | tf_op jit(solution)/shard_map/jit(_take)/select_n | solution.py:82
  51.9 0.7 fusion.22
  52.6 2.1 %fusion.7 = f32[2,15,64,128]{3,2,1,0:T(8,128)} fusion(f32[1,16,64,128]{3,2,1,0:T(8,128)S(1)} %bitcast.78, f32[1,16,64,128]{3,2,1,0:T(8,128)S(1)} %bitcast.76, f32[15,64,128]{2,1,0:T(8,128)} %fusion.12), kind=kLoop, calls=%fused_computation.26 | loop fusion | flops 983040 | bytes 2523136 | tf_op jit(solution)/shard_map/mul | solution.py:145
  54.7 0.7 fusion.19
  55.4 30.3 %all-reduce.2 = (f32[]{:T(128)}, f32[]{:T(128)}, f32[]{:T(128)}, f32[]{:T(128)}) all-reduce(f32[]{:T(128)} %get-tuple-element.3, f32[]{:T(128)} %get-tuple-element.4, f32[]{:T(128)} %get-tuple-element.5, f32[]{:T(128)} %get-tuple-element.2), channel_id=1, replica_groups=mesh['groups'=2,'gx'=4,'gy'=4] {'gx','gy'}, use_global_device_ids=true, to_apply=%region_5.0 | all-reduce | flops 4 | bytes 32 | tf_op jit(solution)/shard_map/psum | solution.py:59
  88.9 3.0 %copy.162 = f32[65,64,1]{2,0,1:T(8,128)} copy(f32[65,64,1]{0,1,2:T(8,128)} %collective-permute-done) | data formatting | bytes 33280 | tf_op jit(solution)/shard_map/ppermute | solution.py:20
  91.9 3.0 %copy.163 = f32[65,64,1]{2,0,1:T(8,128)} copy(f32[65,64,1]{0,1,2:T(8,128)} %collective-permute-done.1) | data formatting | bytes 33280 | tf_op jit(solution)/shard_map/ppermute | solution.py:22
  94.9 1.5 %pad_maximum_fusion.8 = f32[1,64,130]{2,0,1:T(1,128)S(1)} fusion(f32[65,64,1]{2,0,1:T(8,128)} %copy.163, f32[65,64,128]{2,0,1:T(8,128)S(1)} %dynamic-update-slice.4, f32[65,64,1]{2,0,1:T(8,128)} %copy.162), kind=kLoop, calls=%fused_computation.48 | loop fusion | flops 16640 | bytes 2196480 | tf_op jit(solution)/shard_map/slice | solution.py:101
  96.4 0.4 copy-done
  96.8 0.7 copy-done.1
  97.5 0.9 pad_maximum_fusion
  99.2 1.2 %copy.167 = f32[32,64,130]{2,1,0:T(8,128)S(1)} copy(f32[32,64,130]{2,0,1:T(8,128)S(1)} %pad_maximum_fusion) | data formatting | bytes 2129920 | tf_op jit(solution)/shard_map/slice | solution.py:40
  100.5 0.6 copy.169
  101.1 0.6 copy.166
  101.8 1.1 subtract_multiply_fusion
  102.9 0.7 slice_bitcast_fusion.4
  103.6 0.7 slice_bitcast_fusion.8
  104.3 0.7 pad_maximum_fusion.10
  105.3 0.8 broadcast_maximum_fusion.1
  106.6 0.9 pad_maximum_fusion.4
  107.6 0.7 subtract_multiply_fusion.1
  109.0 0.7 fusion
  109.7 0.8 slice_bitcast_fusion
  110.6 0.8 pad_maximum_fusion.7
  (61 shorter events, 3.3 us)
Async XLA Ops:
  0.6 2.3 %copy-start.8 = (f32[2,16,64,128]{3,2,1,0:T(8,128)S(1)}, f32[2,16,64,128]{3,2,1,0:T(8,128)}, u32[]{:S(2)}) copy-start(f32[2,16,64,128]{3,2,1,0:T(8,128)} %param.10) | copy-start | bytes 3145732
  0.6 2.4 %copy-start.2 = (f32[16,64,128]{2,1,0:T(8,128)S(1)}, f32[16,64,128]{2,1,0:T(8,128)}, u32[]{:S(2)}) copy-start(f32[16,64,128]{2,1,0:T(8,128)} %param.9) | copy-start | bytes 1572868
  3.0 1.8 %copy-start.5 = (f32[1,16,64,128]{3,2,1,0:T(8,128)}, f32[1,16,64,128]{3,2,1,0:T(8,128)S(1)}, u32[]{:S(2)}) copy-start(f32[1,16,64,128]{3,2,1,0:T(8,128)S(1)} %get-tuple-element.19) | copy-start | bytes 1572868
  3.0 1.8 %copy-start.11 = (s32[64,128]{1,0:T(8,128)S(1)}, s32[64,128]{1,0:T(8,128)}, u32[]{:S(2)}) copy-start(s32[64,128]{1,0:T(8,128)} %param.11) | copy-start | bytes 98308
  3.0 1.8 %copy-start.13 = (s32[64,128]{1,0:T(8,128)S(1)}, s32[64,128]{1,0:T(8,128)}, u32[]{:S(2)}) copy-start(s32[64,128]{1,0:T(8,128)} %param.12) | copy-start | bytes 98308
  11.0 15.1 %copy-start.14 = (s32[128]{0:T(128)S(1)}, s32[128]{0:T(128)}, u32[]{:S(2)}) copy-start(s32[128]{0:T(128)} %param.15) | copy-start | bytes 1540
  11.0 16.3 %copy-start.3 = (f32[16,64,128]{2,1,0:T(8,128)S(1)}, f32[16,64,128]{2,1,0:T(8,128)}, u32[]{:S(2)}) copy-start(f32[16,64,128]{2,1,0:T(8,128)} %param.8) | copy-start | bytes 1572868
  11.0 77.9 %collective-permute-start = (f32[65,64,1]{0,1,2:T(8,128)}, f32[65,64,1]{0,1,2:T(8,128)}, u32[]{:S(2)}, u32[]{:S(2)}) collective-permute-start(f32[65,64,1]{0,1,2:T(8,128)} %copy.160), channel_id=1, source_target_pairs={{0,4},{4,8},{8,12},{12,0},{1,5},{5,9},{9,13},{13,1},{2,6},{6,10},{... | collective-permute-start | bytes 49928 | tf_op jit(solution)/shard_map/ppermute | solution.py:20
  17.1 74.8 %collective-permute-start.1 = (f32[65,64,1]{0,1,2:T(8,128)}, f32[65,64,1]{0,1,2:T(8,128)}, u32[]{:S(2)}, u32[]{:S(2)}) collective-permute-start(f32[65,64,1]{0,1,2:T(8,128)} %copy.161), channel_id=1, source_target_pairs={{4,0},{8,4},{12,8},{0,12},{5,1},{9,5},{13,9},{1,13},{6,2},{10,6},{... | collective-permute-start | bytes 49928 | tf_op jit(solution)/shard_map/ppermute | solution.py:22
  19.8 83.1 %collective-permute-start.2 = (f32[65,1,128]{2,0,1:T(8,128)}, f32[65,1,128]{2,0,1:T(8,128)}, u32[]{:S(2)}, u32[]{:S(2)}) collective-permute-start(f32[65,1,128]{2,0,1:T(8,128)} %get-tuple-element.17), channel_id=1, source_target_pairs={{1,0},{2,1},{3,2},{5,4},{6,5},{7,6},{9,8},{10,9},{11,10},{13,12},{... | collective-permute-start | bytes 99848 | tf_op jit(solution)/shard_map/ppermute | solution.py:22
  21.1 83.2 %collective-permute-start.3 = (f32[65,1,128]{2,0,1:T(8,128)}, f32[65,1,128]{2,0,1:T(8,128)}, u32[]{:S(2)}, u32[]{:S(2)}) collective-permute-start(f32[65,1,128]{2,0,1:T(8,128)} %get-tuple-element.16), channel_id=1, source_target_pairs={{0,1},{1,2},{2,3},{4,5},{5,6},{6,7},{8,9},{9,10},{10,11},{12,13},{... | collective-permute-start | bytes 99848 | tf_op jit(solution)/shard_map/ppermute | solution.py:20
  26.1 3.8 %copy-start.9 = (f32[1,16,64,128]{3,1,2,0:T(8,128)}, f32[1,16,64,128]{3,1,2,0:T(8,128)S(1)}, u32[]{:S(2)}) copy-start(f32[1,16,64,128]{3,1,2,0:T(8,128)S(1)} %copy.203) | copy-start | bytes 1572868
  47.7 7.0 %copy-start.10 = (f32[64,128]{1,0:T(8,128)S(1)}, f32[64,128]{1,0:T(8,128)}, u32[]{:S(2)}) copy-start(f32[64,128]{1,0:T(8,128)} %param.14) | copy-start | bytes 98308
  94.9 1.8 %copy-start = (f32[65,64,1]{2,0,1:T(8,128)S(1)}, f32[65,64,1]{2,0,1:T(8,128)}, u32[]{:S(2)}) copy-start(f32[65,64,1]{2,0,1:T(8,128)} %copy.162) | copy-start | bytes 49924
  94.9 2.5 %copy-start.1 = (f32[65,64,1]{2,0,1:T(8,128)S(1)}, f32[65,64,1]{2,0,1:T(8,128)}, u32[]{:S(2)}) copy-start(f32[65,64,1]{2,0,1:T(8,128)} %copy.163) | copy-start | bytes 49924
  101.8 2.5 %slice-start = ((f32[49,128]{1,0:T(8,128)}), f32[32,128]{1,0:T(8,128)S(1)}, s32[]{:S(2)}) async-start(f32[49,128]{1,0:T(8,128)} %select_bitcast_fusion), calls=%async_computation | async-start | bytes 32768 | tf_op jit(solution)/shard_map/slice | solution.py:84
  101.8 2.5 %slice-start.1 = ((f32[49,128]{1,0:T(8,128)}), f32[1,128]{1,0:T(1,128)S(1)}, s32[]{:S(2)}) async-start(f32[49,128]{1,0:T(8,128)} %select_bitcast_fusion), calls=%async_computation.1 | async-start | bytes 1024 | tf_op jit(solution)/shard_map/slice | solution.py:84
  104.3 1.1 copy-start.12
  106.4 1.2 %copy-start.6 = (f32[32,64,128]{2,1,0:T(8,128)S(1)}, f32[32,64,128]{2,1,0:T(8,128)}, u32[]{:S(2)}) copy-start(f32[32,64,128]{2,1,0:T(8,128)} %pad_maximum_fusion.6) | copy-start | bytes 3145732
  106.4 1.2 %slice-start.2 = ((f32[33,128]{1,0:T(8,128)}), f32[32,128]{1,0:T(8,128)S(1)}, s32[]{:S(2)}) async-start(f32[33,128]{1,0:T(8,128)} %copy-done.12), calls=%async_computation.2 | async-start | bytes 32768 | tf_op jit(solution)/shard_map/slice | solution.py:114
  107.6 1.0 copy-start.4
  107.6 1.4 %copy-start.7 = (f32[2,15,64,128]{3,2,1,0:T(8,128)S(1)}, f32[2,15,64,128]{3,2,1,0:T(8,128)}, u32[]{:S(2)}) copy-start(f32[2,15,64,128]{3,2,1,0:T(8,128)} %fusion.7) | copy-start | bytes 2949124
where the time goes:
time: 112 us; the launch traced here: 111 us
  blocking collectives  43.6 us (39%)
  local copies, waits for them, and re-layouts  32.9 us (29%)
  other arithmetic  20.6 us (18%)
  starting transfers between devices  10.1 us (9%)
  between operations  4.18 us (4%)
    psum x1, blocking collectives, shards(): lax.psum((jnp.sum(wet_area), jnp.sum(wet_area * rainfall_input), jnp.sum(...  30.3 us
    all_gather x1, blocking collectives, shards(): gathered = lax.all_gather(top_row, 'gx', axis=1, tiled=True)  13.3 us
    unnamed x37, local copies, waits for them, and re-layouts  7.21 us
    ppermute x2, starting transfers between devices, with_halo(): lax.ppermute(tail, axis, [(i, (i + 1) % count) for i in range(ends)])  6.7 us
    slice x3, local copies, waits for them, and re-layouts, with_halo(): lax.slice_in_dim(cells, cells.shape[dim] - width, cells.shape[dim], axis=...  6.57 us
    mul x2, other arithmetic, shards(): wet_cells[:-1] * wet_cells[1:] * vertical_mixing  4.14 us
    ppermute x2, starting transfers between devices, with_halo(): lax.ppermute(head, axis, [((i + 1) % count, i) for i in range(ends)])  3.37 us
    slice x1, local copies, waits for them, and re-layouts, with_halo(): head = lax.slice_in_dim(cells, 0, width, axis=dim)  3.07 us
  transfers between devices with their start and end apart: 4, of which 0 were waited for; matrix products, arithmetic and copies ran while one was open for 32% of the time, Pallas kernels for 0%

commit v1 on v0

--- a/solution.py
+++ b/solution.py
@@ -78,7 +78,7 @@
         ],
         axis=0,
     )
-    gathered = lax.all_gather(top_row, "gx", axis=1, tiled=True)
+    gathered = jnp.concatenate(lax.all_gather(top_row, "gx"), axis=1)
     partner_row = jnp.take(gathered, seam_partner_index, axis=1)
     partner_fields = jnp.concatenate(
         [partner_row[: 2 * layer_stack_number], partner_row[3 * layer_stack_number :]], axis=0

time: 112 us -> 106 us (0.946)
  local copies, waits for them, and re-layouts: 32.9 us -> 26.9 us
  blocking collectives: 43.6 us -> 45.9 us
  starting transfers between devices: 10.1 us -> 8.69 us
    ppermute x2, starting transfers between devices: 6.7 us -> 2.99 us  [with_halo(): lax.ppermute(tail, axis, [(i, (i + 1) % count) for i in range(ends)])]
    unnamed x37 -> x38, local copies, waits for them, and re-layouts: 7.21 us -> 4.14 us
    ppermute x2, starting transfers between devices: 3.37 us -> 5.7 us  [with_halo(): lax.ppermute(head, axis, [((i + 1) % count, i) for i in range(ends)])]
    psum x1, blocking collectives: 30.3 us -> 32.4 us  [shards(): lax.psum((jnp.sum(wet_area), jnp.sum(wet_area * rainfall_input), jnp.sum(...]
    concatenate x2, other arithmetic: 1.83 us -> 3.49 us  [with_halo(): jnp.concatenate([lax.ppermute(tail, axis, [(i, (i + 1) % count) for i in...]
    gather x2, local copies, waits for them, and re-layouts: 2.28 us -> 0.72 us  [shards(): partner_row = jnp.take(gathered, seam_partner_index, axis=1)]
    slice x2 -> x1, other arithmetic: 2.16 us -> 0.74 us  [shards(): north_speed[:, :-1, :]]
    slice x1 -> x2, local copies, waits for them, and re-layouts: 3.07 us -> 4.04 us  [with_halo(): head = lax.slice_in_dim(cells, 0, width, axis=dim)]
  transfers between devices with their start and end apart: 4 -> 4, of which waited for: 0 -> 0; matrix products, arithmetic and copies ran while one was open for 32% -> 34% of each run, Pallas kernels for 0% -> 0%
where the time goes in v1:
time: 106 us; the launch traced here: 105 us
  blocking collectives  45.9 us (43%)
  local copies, waits for them, and re-layouts  26.9 us (25%)
  other arithmetic  19.7 us (19%)
  starting transfers between devices  8.69 us (8%)
  between operations  4.33 us (4%)
    psum x1, blocking collectives, shards(): lax.psum((jnp.sum(wet_area), jnp.sum(wet_area * rainfall_input), jnp.sum(...  32.4 us
    all_gather x1, blocking collectives, shards(): gathered = jnp.concatenate(lax.all_gather(top_row, 'gx'), axis=1)  13.5 us
    slice x2, local copies, waits for them, and re-layouts, with_halo(): lax.slice_in_dim(cells, cells.shape[dim] - width, cells.shape[dim], axis=...  6.18 us
    ppermute x2, starting transfers between devices, with_halo(): lax.ppermute(head, axis, [((i + 1) % count, i) for i in range(ends)])  5.7 us
    mul x2, other arithmetic, shards(): wet_cells[:-1] * wet_cells[1:] * vertical_mixing  4.18 us
    unnamed x38, local copies, waits for them, and re-layouts  4.14 us
    slice x2, local copies, waits for them, and re-layouts, with_halo(): head = lax.slice_in_dim(cells, 0, width, axis=dim)  4.04 us
    ppermute x1, local copies, waits for them, and re-layouts, with_halo(): lax.ppermute(head, axis, [((i + 1) % count, i) for i in range(ends)])  3.78 us
  transfers between devices with their start and end apart: 4, of which 0 were waited for; matrix products, arithmetic and copies ran while one was open for 34% of the time, Pallas kernels for 0%

profile of v1, /device:TPU:0, one launch (start us, length us, event | category | flops | bytes accessed | tf_op | source)
XLA Modules:
  0.0 105.5 jit_solution(128760723017248713)
XLA Ops:
  0.7 1.2 %constant_dynamic-update-slice_fusion.2 = f32[65,64,128]{2,1,0:T(8,128)S(1)} fusion(f32[16,64,128]{2,1,0:T(8,128)} %param.8), kind=kLoop, calls=%fused_computation.71 | loop fusion | bytes 1048576
  1.8 1.1 %constant_dynamic-update-slice_fusion.1 = f32[65,64,128]{2,1,0:T(8,128)S(1)} fusion(f32[65,64,128]{2,1,0:T(8,128)S(1)} %constant_dynamic-update-slice_fusion.2, f32[16,64,128]{2,1,0:T(8,128)} %param.9), kind=kLoop, calls=%fused_computation.70 | loop fusion | bytes 1048576
  3.1 0.7 fusion.24
  3.8 3.0 %collective-permute-start.3 = (f32[65,1,128]{2,1,0:T(1,128)}, f32[65,1,128]{2,1,0:T(1,128)}, u32[]{:S(2)}, u32[]{:S(2)}) collective-permute-start(f32[65,1,128]{2,1,0:T(1,128)} %get-tuple-element.17), channel_id=1, source_target_pairs={{0,1},{1,2},{2,3},{4,5},{5,6},{6,7},{8,9},{9,10},{10,11},{12,13},{... | collective-permute-start | bytes 99848 | tf_op jit(solution)/shard_map/ppermute | solution.py:20
  6.7 1.3 %collective-permute-start.2 = (f32[65,1,128]{2,1,0:T(1,128)}, f32[65,1,128]{2,1,0:T(1,128)}, u32[]{:S(2)}, u32[]{:S(2)}) collective-permute-start(f32[65,1,128]{2,1,0:T(1,128)} %get-tuple-element.16), channel_id=1, source_target_pairs={{1,0},{2,1},{3,2},{5,4},{6,5},{7,6},{9,8},{10,9},{11,10},{13,12},{... | collective-permute-start | bytes 99848 | tf_op jit(solution)/shard_map/ppermute | solution.py:22
  8.0 2.8 %fusion.23 = (f32[65,64,1]{2,1,0:T(8,128)}, f32[65,64,1]{2,1,0:T(8,128)}) fusion(f32[65,64,128]{2,1,0:T(8,128)S(1)} %get-tuple-element.12), kind=kLoop, calls=%fused_computation.80 | loop fusion | bytes 66560 | tf_op jit(solution)/shard_map/slice | solution.py:17
  10.9 3.4 %copy.92 = f32[65,64,1]{0,1,2:T(8,128)} copy(f32[65,64,1]{2,1,0:T(8,128)} %get-tuple-element.15) | data formatting | bytes 33280 | tf_op jit(solution)/shard_map/slice | solution.py:16
  14.2 4.4 %collective-permute-start.1 = (f32[65,64,1]{0,1,2:T(8,128)}, f32[65,64,1]{0,1,2:T(8,128)}, u32[]{:S(2)}, u32[]{:S(2)}) collective-permute-start(f32[65,64,1]{0,1,2:T(8,128)} %copy.92), channel_id=1, source_target_pairs={{4,0},{8,4},{12,8},{0,12},{5,1},{9,5},{13,9},{1,13},{6,2},{10,6},{... | collective-permute-start | bytes 49928 | tf_op jit(solution)/shard_map/ppermute | solution.py:22
  18.7 3.3 %copy.91 = f32[65,64,1]{0,1,2:T(8,128)} copy(f32[65,64,1]{2,1,0:T(8,128)} %get-tuple-element.14) | data formatting | bytes 33280 | tf_op jit(solution)/shard_map/slice | solution.py:17
  22.0 1.1 %slice_bitcast_fusion.1 = f32[16,64,128]{2,1,0:T(8,128)S(1)} fusion(f32[2,16,64,128]{3,2,1,0:T(8,128)} %param.10), kind=kLoop, calls=%fused_computation.38 | loop fusion | bytes 1048576 | tf_op jit(solution)/shard_map/squeeze | solution.py:93
  23.2 0.5 compare_select_fusion
  23.7 0.6 compare_and_fusion
  24.3 1.1 %pad_maximum_fusion.6 = f32[32,64,128]{2,1,0:T(8,128)} fusion(f32[16,64,128]{2,1,0:T(8,128)S(1)} %copy-done.2, f32[16,64,128]{2,1,0:T(8,128)S(1)} %copy-done.3), kind=kLoop, calls=%fused_computation.21 | loop fusion | flops 262144 | bytes 2097152 | tf_op jit(solution)/shard_map/concatenate | solution.py:88
  25.4 0.8 fusion.9
  26.2 13.5 %all-gather.1 = f32[4,49,128]{2,1,0:T(8,128)S(1)} all-gather(f32[1,49,128]{2,1,0:T(8,128)S(1)} %maximum_bitcast_fusion.2), channel_id=2, replica_groups=mesh['groups'=2,'gx'=4,'gy'=4] {'gx'}, dimensions={0}, use_global_device_ids=true | all-gather | bytes 125440 | tf_op jit(solution)/shard_map/all_gather | solution.py:81
  39.8 0.1 copy.98
  39.9 0.7 pad_clamp_fusion
  40.6 0.6 gather_fusion
  41.3 2.1 %fusion.10 = f32[15,64,128]{2,1,0:T(8,128)} fusion(f32[16,64,128]{2,1,0:T(8,128)} %fusion.9), kind=kLoop, calls=%fused_computation.43 | loop fusion | flops 245760 | bytes 1474560 | tf_op jit(solution)/shard_map/mul | solution.py:145
  43.4 0.8 convert_multiply_fusion
  44.2 0.7 select_bitcast_fusion
  44.8 0.7 fusion.22
  45.5 2.1 %fusion.7 = f32[2,15,64,128]{3,2,1,0:T(8,128)} fusion(f32[1,16,64,128]{3,2,1,0:T(8,128)S(1)} %bitcast.74, f32[1,16,64,128]{3,2,1,0:T(8,128)S(1)} %bitcast.72, f32[15,64,128]{2,1,0:T(8,128)} %fusion.10), kind=kLoop, calls=%fused_computation.26 | loop fusion | flops 983040 | bytes 2523136 | tf_op jit(solution)/shard_map/mul | solution.py:145
  47.7 0.7 fusion.19
  48.4 32.4 %all-reduce.2 = (f32[]{:T(128)}, f32[]{:T(128)}, f32[]{:T(128)}, f32[]{:T(128)}) all-reduce(f32[]{:T(128)} %get-tuple-element.3, f32[]{:T(128)} %get-tuple-element.4, f32[]{:T(128)} %get-tuple-element.5, f32[]{:T(128)} %get-tuple-element.2), channel_id=1, replica_groups=mesh['groups'=2,'gx'=4,'gy'=4] {'gx','gy'}, use_global_device_ids=true, to_apply=%region_5.0 | all-reduce | flops 4 | bytes 32 | tf_op jit(solution)/shard_map/psum | solution.py:59
  84.0 3.8 %copy.94 = f32[65,64,1]{2,1,0:T(8,128)} copy(f32[65,64,1]{0,1,2:T(8,128)} %collective-permute-done.1) | data formatting | bytes 33280 | tf_op jit(solution)/shard_map/ppermute | solution.py:22
  87.8 3.7 %copy.93 = f32[65,64,1]{2,1,0:T(8,128)} copy(f32[65,64,1]{0,1,2:T(8,128)} %collective-permute-done) | data formatting | bytes 33280 | tf_op jit(solution)/shard_map/ppermute | solution.py:20
  91.5 2.6 %pad_maximum_fusion = f32[32,64,130]{2,1,0:T(8,128)S(1)} fusion(f32[65,64,1]{2,1,0:T(8,128)} %copy.94, f32[65,64,128]{2,1,0:T(8,128)S(1)} %get-tuple-element.12, f32[65,64,1]{2,1,0:T(8,128)} %copy.93), kind=kLoop, calls=%fused_computation.1 | loop fusion | flops 532480 | bytes 3228160 | tf_op jit(solution)/shard_map/concatenate | solution.py:18
  94.1 0.3 copy-done.1
  94.5 0.3 broadcast_maximum_fusion
  95.0 0.4 slice_multiply_fusion
  95.4 1.1 %subtract_multiply_fusion = f32[2,16,64,129]{3,2,1,0:T(8,128)S(1)} fusion(f32[2,16,64,130]{3,2,1,0:T(8,128)S(1)} %bitcast.71, f32[16,64,129]{2,1,0:T(8,128)S(1)} %get-tuple-element.23, f32[16,64,129]{2,1,0:T(8,128)S(1)} %get-tuple-element.10, f32[16,64,129]{2,1,0:T(8,128)S(1)} %get-tuple-element.22), kind=kLoop, calls=%fused_computation.3 | loop fusion | flops 1849344 | bytes 4755456 | tf_op jit(solution)/shard_map/mul | solution.py:31
  96.5 0.6 slice_bitcast_fusion.5
  97.1 0.7 slice.188
  97.8 0.7 pad_maximum_fusion.8
  98.6 0.3 copy.101
  99.0 0.2 copy.105
  99.2 0.2 copy.102
  99.4 0.3 copy-done.9
  99.7 0.7 maximum_bitcast_fusion.1
  100.5 0.2 copy.100
  100.6 0.9 pad_maximum_fusion.3
  101.7 0.3 subtract_multiply_fusion.1
  102.0 0.8 copy-done.4
  102.7 0.3 copy-done.6
  103.0 0.7 fusion
  103.7 0.8 slice_bitcast_fusion
  104.6 0.8 pad_maximum_fusion.9
  (60 shorter events, 0.8 us)
Async XLA Ops:
  0.6 2.3 %copy-start.7 = (f32[2,16,64,128]{3,2,1,0:T(8,128)S(1)}, f32[2,16,64,128]{3,2,1,0:T(8,128)}, u32[]{:S(2)}) copy-start(f32[2,16,64,128]{3,2,1,0:T(8,128)} %param.10) | copy-start | bytes 3145732
  0.6 2.4 %copy-start.11 = (s32[64,128]{1,0:T(8,128)S(1)}, s32[64,128]{1,0:T(8,128)}, u32[]{:S(2)}) copy-start(s32[64,128]{1,0:T(8,128)} %param.11) | copy-start | bytes 98308
  0.7 2.4 %copy-start.15 = (s32[64,128]{1,0:T(8,128)S(1)}, s32[64,128]{1,0:T(8,128)}, u32[]{:S(2)}) copy-start(s32[64,128]{1,0:T(8,128)} %param.12) | copy-start | bytes 98308
  3.1 22.3 %copy-start.8 = (f32[64,128]{1,0:T(8,128)}, f32[64,128]{1,0:T(8,128)S(1)}, u32[]{:S(2)}) copy-start(f32[64,128]{1,0:T(8,128)S(1)} %get-tuple-element.13) | copy-start | bytes 98308
  3.8 94.1 %collective-permute-start.3 = (f32[65,1,128]{2,1,0:T(1,128)}, f32[65,1,128]{2,1,0:T(1,128)}, u32[]{:S(2)}, u32[]{:S(2)}) collective-permute-start(f32[65,1,128]{2,1,0:T(1,128)} %get-tuple-element.17), channel_id=1, source_target_pairs={{0,1},{1,2},{2,3},{4,5},{5,6},{6,7},{8,9},{9,10},{10,11},{12,13},{... | collective-permute-start | bytes 99848 | tf_op jit(solution)/shard_map/ppermute | solution.py:20
  6.7 89.7 %collective-permute-start.2 = (f32[65,1,128]{2,1,0:T(1,128)}, f32[65,1,128]{2,1,0:T(1,128)}, u32[]{:S(2)}, u32[]{:S(2)}) collective-permute-start(f32[65,1,128]{2,1,0:T(1,128)} %get-tuple-element.16), channel_id=1, source_target_pairs={{1,0},{2,1},{3,2},{5,4},{6,5},{7,6},{9,8},{10,9},{11,10},{13,12},{... | collective-permute-start | bytes 99848 | tf_op jit(solution)/shard_map/ppermute | solution.py:22
  14.2 8.9 %copy-start.2 = (f32[16,64,128]{2,1,0:T(8,128)S(1)}, f32[16,64,128]{2,1,0:T(8,128)}, u32[]{:S(2)}) copy-start(f32[16,64,128]{2,1,0:T(8,128)} %param.9) | copy-start | bytes 1572868
  14.2 8.9 %copy-start.3 = (f32[16,64,128]{2,1,0:T(8,128)S(1)}, f32[16,64,128]{2,1,0:T(8,128)}, u32[]{:S(2)}) copy-start(f32[16,64,128]{2,1,0:T(8,128)} %param.8) | copy-start | bytes 1572868
  14.2 8.9 %copy-start.16 = (s32[128]{0:T(128)S(1)}, s32[128]{0:T(128)}, u32[]{:S(2)}) copy-start(s32[128]{0:T(128)} %param.15) | copy-start | bytes 1540
  14.2 69.8 %collective-permute-start.1 = (f32[65,64,1]{0,1,2:T(8,128)}, f32[65,64,1]{0,1,2:T(8,128)}, u32[]{:S(2)}, u32[]{:S(2)}) collective-permute-start(f32[65,64,1]{0,1,2:T(8,128)} %copy.92), channel_id=1, source_target_pairs={{4,0},{8,4},{12,8},{0,12},{5,1},{9,5},{13,9},{1,13},{6,2},{10,6},{... | collective-permute-start | bytes 49928 | tf_op jit(solution)/shard_map/ppermute | solution.py:22
  22.0 65.8 %collective-permute-start = (f32[65,64,1]{0,1,2:T(8,128)}, f32[65,64,1]{0,1,2:T(8,128)}, u32[]{:S(2)}, u32[]{:S(2)}) collective-permute-start(f32[65,64,1]{0,1,2:T(8,128)} %copy.91), channel_id=1, source_target_pairs={{0,4},{4,8},{8,12},{12,0},{1,5},{5,9},{9,13},{13,1},{2,6},{6,10},{... | collective-permute-start | bytes 49928 | tf_op jit(solution)/shard_map/ppermute | solution.py:20
  26.2 13.5 %copy-start.13 = (f32[16,1,128]{2,1,0:T(1,128)}, f32[16,1,128]{2,1,0:T(1,128)S(1)}, u32[]{:S(2)}) copy-start(f32[16,1,128]{2,1,0:T(1,128)S(1)} %slice.183) | copy-start | bytes 24580
  41.3 6.4 %copy-start.10 = (f32[64,128]{1,0:T(8,128)S(1)}, f32[64,128]{1,0:T(8,128)}, u32[]{:S(2)}) copy-start(f32[64,128]{1,0:T(8,128)} %param.14) | copy-start | bytes 98308
  44.8 43.0 %copy-start.12 = (f32[49,128]{1,0:T(8,128)}, f32[49,128]{1,0:T(8,128)S(1)}, u32[]{:S(2)}) copy-start(f32[49,128]{1,0:T(8,128)S(1)} %select_bitcast_fusion) | copy-start | bytes 75268
  91.5 2.6 %copy-start = (f32[65,64,1]{2,1,0:T(8,128)S(1)}, f32[65,64,1]{2,1,0:T(8,128)}, u32[]{:S(2)}) copy-start(f32[65,64,1]{2,1,0:T(8,128)} %copy.93) | copy-start | bytes 49924
  91.5 2.9 %copy-start.1 = (f32[65,64,1]{2,1,0:T(8,128)S(1)}, f32[65,64,1]{2,1,0:T(8,128)}, u32[]{:S(2)}) copy-start(f32[65,64,1]{2,1,0:T(8,128)} %copy.94) | copy-start | bytes 49924
  95.4 2.4 %slice-start = ((f32[49,128]{1,0:T(8,128)}), f32[1,128]{1,0:T(1,128)S(1)}, s32[]{:S(2)}) async-start(f32[49,128]{1,0:T(8,128)} %copy-done.12), calls=%async_computation | async-start | bytes 1024 | tf_op jit(solution)/shard_map/slice | solution.py:84
  95.4 2.4 %slice-start.1 = ((f32[49,128]{1,0:T(8,128)}), f32[32,128]{1,0:T(8,128)S(1)}, s32[]{:S(2)}) async-start(f32[49,128]{1,0:T(8,128)} %copy-done.12), calls=%async_computation.1 | async-start | bytes 32768 | tf_op jit(solution)/shard_map/slice | solution.py:84
  97.8 1.2 %copy-start.14 = (f32[33,128]{1,0:T(8,128)}, f32[33,128]{1,0:T(8,128)S(1)}, u32[]{:S(2)}) copy-start(f32[33,128]{1,0:T(8,128)S(1)} %maximum_select_fusion) | copy-start | bytes 50692
  98.9 0.8 copy-start.9
  99.0 0.7 slice-start.3
  100.4 1.2 %copy-start.5 = (f32[32,64,128]{2,1,0:T(8,128)S(1)}, f32[32,64,128]{2,1,0:T(8,128)}, u32[]{:S(2)}) copy-start(f32[32,64,128]{2,1,0:T(8,128)} %pad_maximum_fusion.6) | copy-start | bytes 3145732
  100.4 1.2 %slice-start.2 = ((f32[33,128]{1,0:T(8,128)}), f32[32,128]{1,0:T(8,128)S(1)}, s32[]{:S(2)}) async-start(f32[33,128]{1,0:T(8,128)} %copy-done.14), calls=%async_computation.2 | async-start | bytes 32768 | tf_op jit(solution)/shard_map/slice | solution.py:114
  101.7 1.0 copy-start.4
  101.7 1.4 %copy-start.6 = (f32[2,15,64,128]{3,2,1,0:T(8,128)S(1)}, f32[2,15,64,128]{3,2,1,0:T(8,128)}, u32[]{:S(2)}) copy-start(f32[2,15,64,128]{3,2,1,0:T(8,128)} %fusion.7) | copy-start | bytes 2949124
